TPU v7x, 8 devices: a whole 2x2x1 slice. The times are simulated.
8 devices in a mesh: dp: 1 (over z), col: 2 (over y), row: 4 (over x, core).
Axes of the slice: x: 2, y: 2, z: 1, core: 2. Of those that a mesh axis runs over, the one named last changes fastest.
Arguments:
- hidden: bfloat16 [64, 4096], P('dp', 'row')
- norm_gain: float32 [4096], P('row')
- w_head: bfloat16 [4096, 32768], P('row', 'col')
Outputs:
- output 1: float32 [64, 32768], P('dp', ('col', 'row'))
- output 2: float32 [64], P('dp')
All inputs are finite; a program needn't handle non-finite values.
Results may differ from a plain program's by a relative error of at most 0.001.
Values sent between devices are 32-bit elements.
A program may use at most 1 GiB of HBM per device.

v0:
```python
import jax
import jax.numpy as jnp
from jax import lax
from jax.sharding import PartitionSpec as P

EPS = 1e-5


def solution(mesh):
    row_count = mesh.shape["row"]

    def local_head(hidden, norm_gain, w_head):
        wide_hidden = hidden.astype(jnp.float32)
        local_sq = jnp.sum(wide_hidden * wide_hidden, axis=-1, keepdims=True)
        total_sq = lax.psum(local_sq, "row")
        mean_sq = total_sq / (hidden.shape[1] * row_count)
        normed = (wide_hidden * lax.rsqrt(mean_sq + EPS) * norm_gain).astype(jnp.bfloat16)
        share_logits = jnp.dot(normed, w_head, preferred_element_type=jnp.float32)
        logits = lax.psum_scatter(share_logits, "row", scatter_dimension=1, tiled=True)
        local_max = jnp.max(logits, axis=-1, keepdims=True)
        global_max = lax.pmax(local_max, ("col", "row"))
        local_mass = jnp.sum(jnp.exp(logits - global_max), axis=-1, keepdims=True)
        total_mass = lax.psum(local_mass, ("col", "row"))
        log_norm = global_max + jnp.log(total_mass)
        return logits - log_norm, log_norm[:, 0]

    return jax.shard_map(
        local_head,
        mesh=mesh,
        in_specs=(P("dp", "row"), P("row"), P("row", "col")),
        out_specs=(P("dp", ("col", "row")), P("dp")),
        check_vma=False,
    )
```

profile of v0, /device:TPU:0, one launch (start us, length us, event | category | flops | bytes accessed | tf_op | source)
XLA Modules:
  0.0 132.5 jit_solution(16962875233676514221)
XLA Ops:
  7.2 0.0 reduce-scatter.2.cloned.1.call-start
  7.2 1.0 fusion
  8.2 8.8 %psum.14 = f32[64,1]{0,1:T(1,128)S(1)} all-reduce(f32[64,1]{0,1:T(1,128)S(1)} %bitcast.12), channel_id=1, replica_groups=mesh['dp'=1,'col'=2,'row'=4] {'row'}, use_global_device_ids=true, to_apply=%region_1.0 | all-reduce | flops 64 | bytes 512 | tf_op jit(solution)/shard_map/psum | solution.py:15
  17.0 18.6 %fusion.3 = f32[64,16384]{1,0:T(8,128)} fusion(bf16[1024,16384]{1,0:T(8,128)(2,1)} %param.5, bf16[64,1024]{1,0:T(8,128)(2,1)} %param.3, f32[1024]{0:T(1024)} %param.4, f32[64]{0:T(128)S(1)} %rsqrt_bitcast_fusion), kind=kOutput, calls=%fused_computation.7 | convolution fusion | flops 2147745792 | bytes 37884160 | tf_op jit(solution)/shard_map/dot_general | solution.py:18
  35.6 0.0 reduce-scatter.2.cloned.1.call-update
  35.6 38.5 %reduce-scatter.2.cloned.1.call-done = f32[64,4096]{1,0:T(8,128)} async-done(((f32[64,16384]{1,0:T(8,128)}), f32[64,4096]{1,0:T(8,128)}) %reduce-scatter.2.cloned.1.call-update) | async-done | bytes 1048592 | tf_op jit(solution)/shard_map/reduce_scatter | solution.py:19
  74.1 1.4 %reduce_max.9 = f32[64]{0:T(128)S(1)} reduce(f32[64,4096]{1,0:T(8,128)} %reduce-scatter.2.cloned.1.call-done, f32[]{:T(128)} %constant.8.clone.1), dimensions={1}, to_apply=%region_3.0 | reduce | flops 262080 | bytes 1048836 | tf_op jit(solution)/shard_map/reduce_max | solution.py:20
  75.5 22.3 %pmax.7 = f32[64,1]{0,1:T(1,128)S(1)} all-reduce(f32[64,1]{0,1:T(1,128)S(1)} %bitcast.10), channel_id=1, replica_groups=mesh['dp'=1,'col'=2,'row'=4] {'col','row'}, use_global_device_ids=true, to_apply=%region_4.0 | all-reduce | flops 64 | bytes 512 | tf_op jit(solution)/shard_map/pmax | solution.py:21
  97.8 1.5 %exponential_reduce_fusion = f32[64]{0:T(128)S(1)} fusion(f32[64,4096]{1,0:T(8,128)} %reduce-scatter.2.cloned.1.call-done, f32[64]{0:T(128)S(1)} %bitcast.9), kind=kLoop, calls=%fused_computation | loop fusion | flops 524224 | bytes 1049088 | tf_op jit(solution)/shard_map/reduce_sum | solution.py:22
  99.3 24.0 %psum.15 = f32[64,1]{0,1:T(1,128)S(1)} all-reduce(f32[64,1]{0,1:T(1,128)S(1)} %bitcast.11), channel_id=1, replica_groups=mesh['dp'=1,'col'=2,'row'=4] {'col','row'}, use_global_device_ids=true, to_apply=%region_6.0 | all-reduce | flops 64 | bytes 512 | tf_op jit(solution)/shard_map/psum | solution.py:23
  123.3 0.0 copy-start
  123.3 2.3 %broadcast_subtract_fusion = f32[64,4096]{1,0:T(8,128)} fusion(f32[64,4096]{1,0:T(8,128)} %reduce-scatter.2.cloned.1.call-done, f32[64]{0:T(128)S(1)} %add_bitcast_fusion), kind=kLoop, calls=%fused_computation.1 | loop fusion | flops 262144 | bytes 2097408 | tf_op jit(solution)/shard_map/sub | solution.py:25
  125.6 0.0 copy-done
  (2 shorter events, 0.0 us)
Async XLA Ops:
  7.2 67.0 %reduce-scatter.2.cloned.1.call-start = ((), (), s32[]{:S(2)}) async-start(), calls=%async_computation.1 | async-start | bytes 5242880 | tf_op jit(solution)/shard_map/reduce_scatter | solution.py:19
  123.3 2.4 %copy-start = (f32[64]{0:T(128)}, f32[64]{0:T(128)S(1)}, u32[]{:S(2)}) copy-start(f32[64]{0:T(128)S(1)} %add_bitcast_fusion) | copy-start | bytes 772
Sparse Core Ops, SparseCore 0:
  35.8 38.3 reduce-scatter.1
where the time goes:
time: 133 us; the launch traced here: 132 us
  blocking collectives  55 us (41%)
  waiting for transfers between devices  38.5 us (29%)
  matrix products  18.6 us (14%)
  between operations  14 us (11%)
  other arithmetic  6.3 us (5%)
    reduce_scatter x1, waiting for transfers between devices, local_head(): lax.psum_scatter(share_logits, 'row', scatter_dimension=1, tiled=True)  38.5 us
    psum x1, blocking collectives, local_head(): total_mass = lax.psum(local_mass, ('col', 'row'))  24 us
    pmax x1, blocking collectives, local_head(): global_max = lax.pmax(local_max, ('col', 'row'))  22.3 us
    dot_general x1, matrix products, local_head(): share_logits = jnp.dot(normed, w_head, preferred_element_type=jnp.float32)  18.6 us
    psum x1, blocking collectives, local_head(): total_sq = lax.psum(local_sq, 'row')  8.75 us
  transfers between devices with their start and end apart: 1, of which 1 were waited for; matrix products, arithmetic and copies ran while one was open for 0% of the time, Pallas kernels for 0%

commit v1 on v0

v1 whole, which is shorter than its diff:
```python
import functools

import jax
import jax.numpy as jnp
from jax import lax
from jax.experimental import pallas as pl
from jax.experimental.pallas import tpu as pltpu
from jax.sharding import PartitionSpec as P

EPS = 1e-5
MESH = pl.DeviceIdType.MESH
LANES = 128
TILE = 256
IN_FLIGHT = 8


def head_kernel(
    hidden_total,
    hidden_ref,
    gain_ref,
    w_ref,
    logits_ref,
    lse_ref,
    col_ref,
    w_buf,
    x_buf,
    sq_send,
    sq_recv,
    pair_send,
    pair_recv,
    cross_send,
    cross_recv,
    mass_send,
    mass_recv,
    max_acc,
    sum_acc,
    w_sem,
    sq_ssem,
    sq_rsem,
    pair_ssem,
    pair_rsem,
    cross_ssem,
    cross_rsem,
    mass_ssem,
    mass_rsem,
):
    dp = lax.axis_index("dp")
    col = lax.axis_index("col")
    row = lax.axis_index("row")
    core = row % 2
    chip = row // 2
    partner = chip * 2 + (1 - core)
    across = (1 - chip) * 2 + core
    diagonal = (1 - chip) * 2 + (1 - core)
    row_peers = [(col, partner), (col, across), (col, diagonal)]
    other = 1 - col
    col_peers = [(other, row), (other, partner), (other, across), (other, diagonal)]
    peers = row_peers + col_peers

    batch = hidden_ref.shape[0]
    block = logits_ref.shape[1]
    tiles = block // TILE

    def where(peer):
        return (dp, peer[0], peer[1])

    barrier = pltpu.get_barrier_semaphore()
    for peer in peers:
        pl.semaphore_signal(barrier, inc=1, device_id=where(peer), device_id_type=MESH)

    def w_copy(k):
        phase = k // (2 * tiles)
        mine = k % 2
        index = (k % (2 * tiles)) // 2
        target_chip = (1 - phase) * (1 - chip) + phase * chip
        target_core = mine * core + (1 - mine) * (1 - core)
        target = target_chip * 2 + target_core
        start = pl.multiple_of(target * block + index * TILE, TILE)
        return pltpu.make_async_copy(w_ref.at[:, pl.ds(start, TILE)], w_buf.at[k], w_sem.at[k])

    def issue(k, carry):
        w_copy(k).start()
        return carry

    lax.fori_loop(0, IN_FLIGHT, issue, 0)

    wide = hidden_ref[...].astype(jnp.float32)
    local_sq = jnp.sum(wide * wide, axis=-1, keepdims=True)
    sq_send[...] = jnp.broadcast_to(local_sq, sq_send.shape)

    pl.semaphore_wait(barrier, len(peers))

    sq_copies = []
    for n, peer in enumerate(row_peers):
        copy = pltpu.make_async_remote_copy(
            src_ref=sq_send,
            dst_ref=sq_recv.at[n],
            send_sem=sq_ssem.at[n],
            recv_sem=sq_rsem.at[n],
            device_id=where(peer),
            device_id_type=MESH,
        )
        copy.start()
        sq_copies.append(copy)
    for copy in sq_copies:
        copy.wait()
    pair_here = sq_send[...] + sq_recv[0]
    pair_there = sq_recv[1] + sq_recv[2]
    total_sq = (pair_here + pair_there)[:, :1]
    inv = lax.rsqrt(total_sq / hidden_total + EPS)
    x_buf[...] = (wide * inv * gain_ref[...]).astype(jnp.bfloat16)

    def product(k):
        w_copy(k).wait()

        @pl.when(k + IN_FLIGHT < 4 * tiles)
        def _():
            w_copy(k + IN_FLIGHT).start()

        return jnp.dot(x_buf[...], w_buf[k], preferred_element_type=jnp.float32)

    def pair_copy(n):
        return pltpu.make_async_remote_copy(
            src_ref=pair_send.at[n],
            dst_ref=pair_recv.at[n],
            send_sem=pair_ssem.at[n],
            recv_sem=pair_rsem.at[n],
            device_id=where((col, partner)),
            device_id_type=MESH,
        )

    def cross_copy(n):
        return pltpu.make_async_remote_copy(
            src_ref=cross_send.at[n],
            dst_ref=cross_recv.at[n],
            send_sem=cross_ssem.at[n],
            recv_sem=cross_rsem.at[n],
            device_id=where((col, across)),
            device_id_type=MESH,
        )

    def outgoing(n, carry):
        pair_send[n] = product(2 * n)
        pair_copy(n).start()
        own = product(2 * n + 1)
        pair_copy(n).wait_recv()
        cross_send[n] = own + pair_recv[n]
        cross_copy(n).start()
        return carry

    lax.fori_loop(0, tiles, outgoing, 0)

    def local(n, carry):
        k = tiles + n
        pair_send[k] = product(2 * k)
        pair_copy(k).start()
        own = product(2 * k + 1)
        pair_copy(k).wait_recv()
        logits_ref[:, pl.ds(pl.multiple_of(n * TILE, TILE), TILE)] = own + pair_recv[k]
        return carry

    lax.fori_loop(0, tiles, local, 0)

    max_acc[...] = jnp.full(max_acc.shape, -jnp.inf, jnp.float32)
    sum_acc[...] = jnp.zeros(sum_acc.shape, jnp.float32)

    def finish(n, carry):
        cross_copy(n).wait_recv()
        columns = pl.ds(pl.multiple_of(n * TILE, TILE), TILE)
        z = logits_ref[:, columns] + cross_recv[n]
        logits_ref[:, columns] = z
        pieces = [z[:, i * LANES : (i + 1) * LANES] for i in range(TILE // LANES)]
        high = functools.reduce(jnp.maximum, pieces, max_acc[...])
        mass = sum_acc[...] * jnp.exp(max_acc[...] - high)
        for piece in pieces:
            mass = mass + jnp.exp(piece - high)
        max_acc[...] = high
        sum_acc[...] = mass
        return carry

    lax.fori_loop(0, tiles, finish, 0)

    high_t = max_acc[...].T
    mass_t = sum_acc[...].T
    high = jnp.max(high_t, axis=0, keepdims=True)
    mass = jnp.sum(mass_t * jnp.exp(high_t - high), axis=0, keepdims=True)
    mass_send[0:1, :] = high
    mass_send[1:2, :] = mass

    mass_copies = []
    for n, peer in enumerate(peers):
        copy = pltpu.make_async_remote_copy(
            src_ref=mass_send,
            dst_ref=mass_recv.at[n],
            send_sem=mass_ssem.at[n],
            recv_sem=mass_rsem.at[n],
            device_id=where(peer),
            device_id_type=MESH,
        )
        copy.start()
        mass_copies.append(copy)
    for n in range(2 * tiles):
        pair_copy(n).wait_send()
    for n in range(tiles):
        cross_copy(n).wait_send()
    for copy in mass_copies:
        copy.wait()
    highs = [high] + [mass_recv[n, 0:1, :] for n in range(len(peers))]
    masses = [mass] + [mass_recv[n, 1:2, :] for n in range(len(peers))]
    top = functools.reduce(jnp.maximum, highs)
    terms = [m * jnp.exp(h - top) for h, m in zip(highs, masses)]
    here = (terms[0] + terms[1]) + (terms[2] + terms[3])
    there = (terms[4] + terms[5]) + (terms[6] + terms[7])
    lse = top + jnp.log(here + there)
    lse_ref[...] = lse
    col_ref[...] = jnp.broadcast_to(lse, (LANES, batch)).T


def solution(mesh):
    row_count = mesh.shape["row"]

    def local_head(hidden, norm_gain, w_head):
        batch, depth = hidden.shape
        block = w_head.shape[1] // row_count
        tiles = block // TILE
        peer_count = 7
        logits, lse, lse_col = pl.pallas_call(
            functools.partial(head_kernel, float(depth * row_count)),
            out_shape=(
                jax.ShapeDtypeStruct((batch, block), jnp.float32),
                jax.ShapeDtypeStruct((1, batch), jnp.float32),
                jax.ShapeDtypeStruct((batch, LANES), jnp.float32),
            ),
            in_specs=[
                pl.BlockSpec(memory_space=pltpu.VMEM),
                pl.BlockSpec(memory_space=pltpu.VMEM),
                pl.BlockSpec(memory_space=pl.ANY),
            ],
            out_specs=(
                pl.BlockSpec(memory_space=pltpu.VMEM),
                pl.BlockSpec(memory_space=pltpu.VMEM),
                pl.BlockSpec(memory_space=pltpu.VMEM),
            ),
            scratch_shapes=[
                pltpu.VMEM((4 * tiles, depth, TILE), jnp.bfloat16),
                pltpu.VMEM((batch, depth), jnp.bfloat16),
                pltpu.VMEM((batch, LANES), jnp.float32),
                pltpu.VMEM((3, batch, LANES), jnp.float32),
                pltpu.VMEM((2 * tiles, batch, TILE), jnp.float32),
                pltpu.VMEM((2 * tiles, batch, TILE), jnp.float32),
                pltpu.VMEM((tiles, batch, TILE), jnp.float32),
                pltpu.VMEM((tiles, batch, TILE), jnp.float32),
                pltpu.VMEM((2, batch), jnp.float32),
                pltpu.VMEM((peer_count, 2, batch), jnp.float32),
                pltpu.VMEM((batch, LANES), jnp.float32),
                pltpu.VMEM((batch, LANES), jnp.float32),
                pltpu.SemaphoreType.DMA((4 * tiles,)),
                pltpu.SemaphoreType.DMA((3,)),
                pltpu.SemaphoreType.DMA((3,)),
                pltpu.SemaphoreType.DMA((2 * tiles,)),
                pltpu.SemaphoreType.DMA((2 * tiles,)),
                pltpu.SemaphoreType.DMA((tiles,)),
                pltpu.SemaphoreType.DMA((tiles,)),
                pltpu.SemaphoreType.DMA((peer_count,)),
                pltpu.SemaphoreType.DMA((peer_count,)),
            ],
            compiler_params=pltpu.CompilerParams(
                collective_id=0, has_side_effects=True, vmem_limit_bytes=56 * 1024 * 1024
            ),
        )(hidden, norm_gain.reshape(1, depth), w_head)
        return logits - lse_col[:, :1], lse[0]

    return jax.shard_map(
        local_head,
        mesh=mesh,
        in_specs=(P("dp", "row"), P("row"), P("row", "col")),
        out_specs=(P("dp", ("col", "row")), P("dp")),
        check_vma=False,
    )
```

time: 133 us -> 69.3 us (0.52)
  Pallas kernels: 0 us -> 64.1 us
  blocking collectives: 55 us -> 0 us
  waiting for transfers between devices: 38.5 us -> 0 us
  matrix products: 18.6 us -> 0 us
  between operations: 14 us -> 0.64 us
  other arithmetic: 6.3 us -> 2.35 us
  local copies, waits for them, and re-layouts: 0.01 us -> 2 us
    pallas_call x0 -> x1, Pallas kernels: none -> 64.1 us  [local_head(): pl.pallas_call(functools.partial(head_kernel, float(depth * row_count)),...]
    reduce_scatter x1 -> x0, waiting for transfers between devices: 38.5 us -> none  [local_head(): lax.psum_scatter(share_logits, 'row', scatter_dimension=1, tiled=True)]
    psum x2 -> x0, blocking collectives: 32.7 us -> none  [the longest x1 24 us: local_head(): total_mass = lax.psum(local_mass, ('col', 'row'))]
    pmax x1 -> x0, blocking collectives: 22.3 us -> none  [local_head(): global_max = lax.pmax(local_max, ('col', 'row'))]
    dot_general x1 -> x0, matrix products: 18.6 us -> none  [local_head(): share_logits = jnp.dot(normed, w_head, preferred_element_type=jnp.float32)]
    reduce_sum x2 -> x0, other arithmetic: 2.57 us -> none  [the longest x1 1.53 us: local_head(): local_mass = jnp.sum(jnp.exp(logits - global_max), axis=-1, keepdims=True)]
    reduce_max x1 -> x0, other arithmetic: 1.38 us -> none  [local_head(): local_max = jnp.max(logits, axis=-1, keepdims=True)]
  transfers between devices with their start and end apart: 1 -> 0, of which waited for: 1 -> 0; matrix products, arithmetic and copies ran while one was open for 0% -> 0% of each run, Pallas kernels for 0% -> 0%
where the time goes in v1:
time: 69.3 us; the launch traced here: 69.1 us
  Pallas kernels  64.1 us (92%)
  other arithmetic  2.35 us (3%)
  local copies, waits for them, and re-layouts  2 us (3%)
    pallas_call x1, Pallas kernels, local_head(): pl.pallas_call(functools.partial(head_kernel, float(depth * row_count)),...  64.1 us
    sub x1, other arithmetic, local_head(): return (logits - lse_col[:, :1], lse[0])  2.35 us

profile of v1, /device:TPU:0, one launch (start us, length us, event | category | flops | bytes accessed | tf_op | source)
XLA Modules:
  0.0 69.1 jit_solution(1484819523427482102)
XLA Ops:
  0.6 64.1 %shard_map.50 = (f32[64,4096]{1,0:T(8,128)}, f32[1,64]{1,0:T(1,128)}, f32[64,128]{1,0:T(8,128)}) custom-call(bf16[64,1024]{1,0:T(8,128)(2,1)} %hidden_ref.1, f32[1,1024]{1,0:T(1,128)} %bitcast.2, bf16[1024,16384]{1,0:T(8,128)(2,1)} %w_ref.1), custom_call_target="tpu_custom_call" | custom-call | tf_op jit(solution)/shard_map/pallas_call | solution.py:227
  64.8 0.9 %slice_reduce_fusion = f32[64]{0:T(128)S(1)} fusion(f32[64,128]{1,0:T(8,128)} %get-tuple-element.6), kind=kLoop, calls=%fused_computation.1 | loop fusion | bytes 512 | tf_op jit(solution)/shard_map/slice | solution.py:271
  65.6 2.3 %broadcast_subtract_fusion = f32[64,4096]{1,0:T(8,128)} fusion(f32[64,4096]{1,0:T(8,128)} %get-tuple-element.5, f32[64]{0:T(128)S(1)} %slice_reduce_fusion), kind=kLoop, calls=%fused_computation | loop fusion | flops 262144 | bytes 2097408 | tf_op jit(solution)/shard_map/sub | solution.py:271
  68.0 1.1 %copy.6 = f32[64]{0:T(128)} copy(f32[64]{0:T(128)} %bitcast.3) | data formatting | bytes 512
